TPU v7x, 256 devices: a whole 4x4x8 slice. The times are simulated.
256 devices in a mesh: section: 16 (over x, y), tensor: 16 (over z, core).
Axes of the slice: x: 4, y: 4, z: 8, core: 2. Of those that a mesh axis runs over, the one named last changes fastest.
Arguments:
- token_ids: int32 [3, 48], replicated, may hold values from 0 to 31999
- emb_table: bfloat16 [32000, 4096], P('section', 'tensor'), may hold values from -6 to 6
- attn_gain: bfloat16 [16, 4096], P('section'), may hold values from 0.25 to 1.75
- query_weight: bfloat16 [16, 4096, 4096], P('section', None, 'tensor'), may hold values from -8 to 8
- key_weight: bfloat16 [16, 4096, 4096], P('section', None, 'tensor'), may hold values from -8 to 8
- value_weight: bfloat16 [16, 4096, 4096], P('section', None, 'tensor'), may hold values from -0.09375 to 0.09375
- mix_weight: float32 [16, 32], P('section', 'tensor'), may hold values from 0.2 to 0.8
- out_weight: bfloat16 [16, 4096, 4096], P('section', 'tensor'), may hold values from -0.125 to 0.125
Outputs:
- layer_outputs: bfloat16 [16, 3, 48, 4096], P('section', None, None, 'tensor')
All inputs are finite; a program needn't handle non-finite values.
Results may differ from a plain program's by a relative error of at most 0.033.
Values may be sent and summed in bfloat16 or wider, within the bound.
No kernel may reach another device: no remote copies, remote signals or barrier semaphores. Data moves between devices by JAX's collectives and lax.ppermute only.
A program may use at most 64 MiB of HBM per device.

v0:
```python
import jax
import jax.numpy as jnp
from jax import lax
from jax.sharding import PartitionSpec as P

EPSILON = 1e-05
ROTARY_BASE = 10000.0


def from_everyone(array, axis):
    peers = lax.axis_size(axis)
    return lax.all_to_all(
        jnp.broadcast_to(array[None], (peers, *array.shape)), axis, 0, 0, tiled=True
    )


def of_everyone(array, axis):
    return from_everyone(array, axis).astype(jnp.float32).sum(axis=0)


def broadcast(array, axis, root):
    return lax.dynamic_index_in_dim(lax.all_gather(array, axis), root, 0, keepdims=False)


def laid_out(pieces, dim):
    lengths = list(pieces.shape[1:])
    lengths[dim] *= pieces.shape[0]
    return jnp.moveaxis(pieces, 0, dim).reshape(lengths)


def gather_directly(array, axis, dim):
    return laid_out(from_everyone(array, axis), dim)


def in_blocks(array, dim, peers):
    lengths = array.shape
    pieces = array.reshape(*lengths[:dim], peers, lengths[dim] // peers, *lengths[dim + 1 :])
    return jnp.moveaxis(pieces, dim, 0)


def summed_on_arrival(array, axis, dim):
    pieces = in_blocks(array, dim, lax.axis_size(axis))
    arrived = lax.all_to_all(pieces, axis, split_axis=0, concat_axis=0, tiled=True)
    return arrived.astype(jnp.float32).sum(axis=0)


def shifted(value, axis, steps):
    count = lax.axis_size(axis)
    first, last = (max(0, -steps), min(count, count - steps))
    return lax.ppermute(value, axis, [(source, source + steps) for source in range(first, last)])


def rms_scale(values, norm_gain):
    mean_square = jnp.mean(values * values, axis=-1, keepdims=True)
    return values * lax.rsqrt(mean_square + EPSILON) * norm_gain


def rotate(values):
    length = values.shape[-3]
    head_dim = values.shape[-1]
    half_dim = head_dim // 2
    positions = jnp.arange(length, dtype=jnp.float32)
    frequency = ROTARY_BASE ** (-(jnp.arange(half_dim, dtype=jnp.float32) * 2.0) / head_dim)
    angles = positions[:, None] * frequency[None, :]
    cosine = jnp.cos(angles)[:, None, :]
    sine_table = jnp.sin(angles)[:, None, :]
    leading = values[..., :half_dim]
    second = values[..., half_dim:]
    return jnp.concatenate(
        [leading * cosine - second * sine_table, second * cosine + leading * sine_table], axis=-1
    )


def attend(queries, key_rows, mixed_values):
    length = queries.shape[0]
    head_dim = queries.shape[2]
    scores = jnp.einsum(
        "qhd,khd->hqk", queries, key_rows, preferred_element_type=jnp.float32
    ) * head_dim ** (-0.5)
    causal = jnp.arange(length)[:, None] >= jnp.arange(length)[None, :]
    scores = jnp.where(causal, scores, -1e30)
    row_top = jnp.max(scores, axis=-1, keepdims=True)
    expo = jnp.exp(scores - row_top)
    attn_probs = (expo / jnp.sum(expo, axis=-1, keepdims=True)).astype(jnp.bfloat16)
    attended = jnp.einsum(
        "hqk,khd->qhd", attn_probs, mixed_values, preferred_element_type=jnp.float32
    )
    return attended.astype(jnp.bfloat16)


def shards(
    token_ids, emb_table, attn_gain, query_weight, key_weight, value_weight, mix_weight, out_weight
):
    section_rank = lax.axis_index("section")
    section_count = lax.axis_size("section")
    batches, length = token_ids.shape
    vocab_local, width_local = emb_table.shape
    head_local = mix_weight.shape[1]
    head_dim = query_weight.shape[2] // head_local
    norm_gain = attn_gain[0].astype(jnp.float32)
    w_query = query_weight[0]
    w_key = key_weight[0]
    w_value = value_weight[0]
    w_out = out_weight[0]
    mix_rate = mix_weight[0][None, :, None]
    flat_ids = token_ids.reshape(-1) - section_rank * vocab_local
    one_hot = (flat_ids[:, None] == jnp.arange(vocab_local, dtype=jnp.int32)[None, :]).astype(
        jnp.bfloat16
    )
    looked = jnp.dot(one_hot, emb_table, preferred_element_type=jnp.float32)
    first_shard = (
        of_everyone(looked.astype(jnp.bfloat16), "section").astype(jnp.float32).astype(jnp.bfloat16)
    )
    first_full = lax.all_gather(first_shard, "tensor", axis=1, tiled=True)
    first_float = first_full.astype(jnp.float32)

    def root_project():
        first_norm = rms_scale(first_float, norm_gain).astype(jnp.bfloat16)
        return jnp.dot(first_norm, w_value, preferred_element_type=jnp.float32).astype(jnp.bfloat16)

    def skipped():
        return jnp.zeros((first_full.shape[0], w_value.shape[1]), jnp.bfloat16)

    own_values = lax.cond(section_rank == 0, root_project, skipped)
    first_values = broadcast(own_values, "section", 0)
    source_values = first_values.reshape(batches, length, head_local, head_dim)
    first_blocks = first_shard.reshape(batches, length, width_local)

    def attention_branch(full_rows, micro_index):
        normed = rms_scale(full_rows.astype(jnp.float32), norm_gain).astype(jnp.bfloat16)
        queries = jnp.dot(normed, w_query, preferred_element_type=jnp.float32)
        key_rows = jnp.dot(normed, w_key, preferred_element_type=jnp.float32)
        values = jnp.dot(normed, w_value, preferred_element_type=jnp.float32)
        queries = rotate(queries.reshape(length, head_local, head_dim)).astype(jnp.bfloat16)
        key_rows = rotate(key_rows.reshape(length, head_local, head_dim)).astype(jnp.bfloat16)
        values = values.reshape(length, head_local, head_dim)
        picked = lax.dynamic_index_in_dim(source_values, micro_index, 0, keepdims=False).astype(
            jnp.float32
        )
        mixed_values = (mix_rate * values + (1.0 - mix_rate) * picked).astype(jnp.bfloat16)
        attended = attend(queries, key_rows, mixed_values).reshape(length, head_local * head_dim)
        return jnp.dot(attended, w_out, preferred_element_type=jnp.float32)

    def advance(step_index, loop_state):
        incoming, outputs = loop_state
        position = step_index - section_rank
        is_valid = (position >= 0) & (position < batches)
        micro_index = jnp.clip(position, 0, batches - 1)
        starting = lax.dynamic_index_in_dim(first_blocks, micro_index, 0, keepdims=False)
        shard_rows = jnp.where(section_rank == 0, starting, incoming)
        full_rows = gather_directly(shard_rows, "tensor", 1)
        summed = summed_on_arrival(
            attention_branch(full_rows, micro_index).astype(jnp.bfloat16), "tensor", 1
        )
        fresh_rows = (shard_rows.astype(jnp.float32) + summed).astype(jnp.bfloat16)
        previous = lax.dynamic_index_in_dim(outputs, micro_index, 0, keepdims=False)
        kept_rows = jnp.where(is_valid, fresh_rows, previous)
        outputs = lax.dynamic_update_index_in_dim(outputs, kept_rows, micro_index, 0)
        incoming = shifted(fresh_rows, "section", 1)
        return (incoming, outputs)

    incoming = jnp.zeros((length, width_local), jnp.bfloat16)
    outputs = jnp.zeros((batches, length, width_local), jnp.bfloat16)
    step_count = batches + section_count - 1
    incoming, outputs = lax.fori_loop(0, step_count, advance, (incoming, outputs))
    return outputs[None]


def solution(mesh):
    in_specs = (
        P(),
        P("section", "tensor"),
        P("section", None),
        P("section", None, "tensor"),
        P("section", None, "tensor"),
        P("section", None, "tensor"),
        P("section", "tensor"),
        P("section", "tensor", None),
    )
    out_specs = P("section", None, None, "tensor")
    return jax.shard_map(shards, mesh=mesh, in_specs=in_specs, out_specs=out_specs, check_vma=False)
```

profile of v0, /device:TPU:1, one launch (start us, length us, event | category | flops | bytes accessed | tf_op | source)
XLA Modules:
  0.0 1193.2 jit_solution(4408953827602636049)
XLA Ops:
  8.2 24.9 %all_to_all.29 = bf16[16,144,256]{2,1,0:T(8,128)(2,1)} all-to-all(bf16[16,144,256]{2,1,0:T(8,128)(2,1)S(1)} %broadcast_in_dim.99), channel_id=1, replica_groups=mesh['section'=16,'tensor'=16] {'section'}, dimensions={0} | all-to-all | bytes 2359296 | tf_op jit(solution)/shard_map/all_to_all | solution.py:12
  38.3 36.1 %all-gather.4.cloned.1.call-done = bf16[144,4096]{1,0:T(8,128)(2,1)} async-done(((bf16[144,256]{1,0:T(8,128)(2,1)}), bf16[144,4096]{1,0:T(8,128)(2,1)}) %all-gather.4.cloned.1.call-update) | async-done | bytes 1179664 | tf_op jit(solution)/shard_map/all_gather | solution.py:114
  89.5 33.5 %all-gather.6.cloned.1.call-done = bf16[2304,256]{1,0:T(8,128)(2,1)} async-done(((bf16[144,256]{1,0:T(8,128)(2,1)}), bf16[2304,256]{1,0:T(8,128)(2,1)}) %all-gather.6.cloned.1.call-update) | async-done | bytes 1179664 | tf_op jit(solution)/shard_map/all_gather | solution.py:22
  125.2 1061.2 %while.17 = (s32[]{:T(128)}, bf16[48,256]{1,0:T(8,128)(2,1)S(1)}, bf16[3,48,256]{2,1,0:T(8,128)(2,1)}, pred[]{:T(512)}, s32[]{:T(128)}, /*index=5*/bf16[3,48,256...) while((s32[]{:T(128)}, bf16[48,256]{1,0:T(8,128)(2,1)S(1)}, ...), condition=%wide.wide.region_9.10_spmd, body=%wide.wide.region_4.9_spmd.sunk | while | flops 407331392 | bytes 26102732 | solution.py:165
  140.0 10.5 all-to-all-done
  169.2 12.5 %all-to-all-done.1 = bf16[16,48,256]{2,1,0:T(8,128)(2,1)S(1)} async-done(((bf16[16,48,256]{2,1,0:T(8,128)(2,1)}), bf16[16,48,256]{2,1,0:T(8,128)(2,1)S(1)}, u32[]{:S(2)}, u32[]{:S(2)}) %all-to-all-start.1) | async-done | bytes 393248 | tf_op jit(solution)/shard_map/while/body/eval_jaxpr/all_to_all | solution.py:43
  196.1 10.5 all-to-all-done
  225.3 12.5 %all-to-all-done.1 = bf16[16,48,256]{2,1,0:T(8,128)(2,1)S(1)} async-done(((bf16[16,48,256]{2,1,0:T(8,128)(2,1)}), bf16[16,48,256]{2,1,0:T(8,128)(2,1)S(1)}, u32[]{:S(2)}, u32[]{:S(2)}) %all-to-all-start.1) | async-done | bytes 393248 | tf_op jit(solution)/shard_map/while/body/eval_jaxpr/all_to_all | solution.py:43
  253.3 10.5 all-to-all-done
  282.5 12.5 %all-to-all-done.1 = bf16[16,48,256]{2,1,0:T(8,128)(2,1)S(1)} async-done(((bf16[16,48,256]{2,1,0:T(8,128)(2,1)}), bf16[16,48,256]{2,1,0:T(8,128)(2,1)S(1)}, u32[]{:S(2)}, u32[]{:S(2)}) %all-to-all-start.1) | async-done | bytes 393248 | tf_op jit(solution)/shard_map/while/body/eval_jaxpr/all_to_all | solution.py:43
  339.7 12.5 %all-to-all-done.1 = bf16[16,48,256]{2,1,0:T(8,128)(2,1)S(1)} async-done(((bf16[16,48,256]{2,1,0:T(8,128)(2,1)}), bf16[16,48,256]{2,1,0:T(8,128)(2,1)S(1)}, u32[]{:S(2)}, u32[]{:S(2)}) %all-to-all-start.1) | async-done | bytes 393248 | tf_op jit(solution)/shard_map/while/body/eval_jaxpr/all_to_all | solution.py:43
  396.9 12.5 %all-to-all-done.1 = bf16[16,48,256]{2,1,0:T(8,128)(2,1)S(1)} async-done(((bf16[16,48,256]{2,1,0:T(8,128)(2,1)}), bf16[16,48,256]{2,1,0:T(8,128)(2,1)S(1)}, u32[]{:S(2)}, u32[]{:S(2)}) %all-to-all-start.1) | async-done | bytes 393248 | tf_op jit(solution)/shard_map/while/body/eval_jaxpr/all_to_all | solution.py:43
  454.2 12.5 %all-to-all-done.1 = bf16[16,48,256]{2,1,0:T(8,128)(2,1)S(1)} async-done(((bf16[16,48,256]{2,1,0:T(8,128)(2,1)}), bf16[16,48,256]{2,1,0:T(8,128)(2,1)S(1)}, u32[]{:S(2)}, u32[]{:S(2)}) %all-to-all-start.1) | async-done | bytes 393248 | tf_op jit(solution)/shard_map/while/body/eval_jaxpr/all_to_all | solution.py:43
  512.8 12.5 %all-to-all-done.1 = bf16[16,48,256]{2,1,0:T(8,128)(2,1)S(1)} async-done(((bf16[16,48,256]{2,1,0:T(8,128)(2,1)}), bf16[16,48,256]{2,1,0:T(8,128)(2,1)S(1)}, u32[]{:S(2)}, u32[]{:S(2)}) %all-to-all-start.1) | async-done | bytes 393248 | tf_op jit(solution)/shard_map/while/body/eval_jaxpr/all_to_all | solution.py:43
  542.9 10.5 all-to-all-done
  572.1 12.5 %all-to-all-done.1 = bf16[16,48,256]{2,1,0:T(8,128)(2,1)S(1)} async-done(((bf16[16,48,256]{2,1,0:T(8,128)(2,1)}), bf16[16,48,256]{2,1,0:T(8,128)(2,1)S(1)}, u32[]{:S(2)}, u32[]{:S(2)}) %all-to-all-start.1) | async-done | bytes 393248 | tf_op jit(solution)/shard_map/while/body/eval_jaxpr/all_to_all | solution.py:43
  602.3 10.5 all-to-all-done
  631.4 12.5 %all-to-all-done.1 = bf16[16,48,256]{2,1,0:T(8,128)(2,1)S(1)} async-done(((bf16[16,48,256]{2,1,0:T(8,128)(2,1)}), bf16[16,48,256]{2,1,0:T(8,128)(2,1)S(1)}, u32[]{:S(2)}, u32[]{:S(2)}) %all-to-all-start.1) | async-done | bytes 393248 | tf_op jit(solution)/shard_map/while/body/eval_jaxpr/all_to_all | solution.py:43
  661.6 10.5 all-to-all-done
  690.8 12.5 %all-to-all-done.1 = bf16[16,48,256]{2,1,0:T(8,128)(2,1)S(1)} async-done(((bf16[16,48,256]{2,1,0:T(8,128)(2,1)}), bf16[16,48,256]{2,1,0:T(8,128)(2,1)S(1)}, u32[]{:S(2)}, u32[]{:S(2)}) %all-to-all-start.1) | async-done | bytes 393248 | tf_op jit(solution)/shard_map/while/body/eval_jaxpr/all_to_all | solution.py:43
  750.1 12.5 %all-to-all-done.1 = bf16[16,48,256]{2,1,0:T(8,128)(2,1)S(1)} async-done(((bf16[16,48,256]{2,1,0:T(8,128)(2,1)}), bf16[16,48,256]{2,1,0:T(8,128)(2,1)S(1)}, u32[]{:S(2)}, u32[]{:S(2)}) %all-to-all-start.1) | async-done | bytes 393248 | tf_op jit(solution)/shard_map/while/body/eval_jaxpr/all_to_all | solution.py:43
  809.4 12.5 %all-to-all-done.1 = bf16[16,48,256]{2,1,0:T(8,128)(2,1)S(1)} async-done(((bf16[16,48,256]{2,1,0:T(8,128)(2,1)}), bf16[16,48,256]{2,1,0:T(8,128)(2,1)S(1)}, u32[]{:S(2)}, u32[]{:S(2)}) %all-to-all-start.1) | async-done | bytes 393248 | tf_op jit(solution)/shard_map/while/body/eval_jaxpr/all_to_all | solution.py:43
  868.8 12.5 %all-to-all-done.1 = bf16[16,48,256]{2,1,0:T(8,128)(2,1)S(1)} async-done(((bf16[16,48,256]{2,1,0:T(8,128)(2,1)}), bf16[16,48,256]{2,1,0:T(8,128)(2,1)S(1)}, u32[]{:S(2)}, u32[]{:S(2)}) %all-to-all-start.1) | async-done | bytes 393248 | tf_op jit(solution)/shard_map/while/body/eval_jaxpr/all_to_all | solution.py:43
  898.9 10.5 all-to-all-done
  928.1 12.5 %all-to-all-done.1 = bf16[16,48,256]{2,1,0:T(8,128)(2,1)S(1)} async-done(((bf16[16,48,256]{2,1,0:T(8,128)(2,1)}), bf16[16,48,256]{2,1,0:T(8,128)(2,1)S(1)}, u32[]{:S(2)}, u32[]{:S(2)}) %all-to-all-start.1) | async-done | bytes 393248 | tf_op jit(solution)/shard_map/while/body/eval_jaxpr/all_to_all | solution.py:43
  958.3 10.5 all-to-all-done
  987.4 12.5 %all-to-all-done.1 = bf16[16,48,256]{2,1,0:T(8,128)(2,1)S(1)} async-done(((bf16[16,48,256]{2,1,0:T(8,128)(2,1)}), bf16[16,48,256]{2,1,0:T(8,128)(2,1)S(1)}, u32[]{:S(2)}, u32[]{:S(2)}) %all-to-all-start.1) | async-done | bytes 393248 | tf_op jit(solution)/shard_map/while/body/eval_jaxpr/all_to_all | solution.py:43
  1017.6 10.5 all-to-all-done
  1046.8 12.5 %all-to-all-done.1 = bf16[16,48,256]{2,1,0:T(8,128)(2,1)S(1)} async-done(((bf16[16,48,256]{2,1,0:T(8,128)(2,1)}), bf16[16,48,256]{2,1,0:T(8,128)(2,1)S(1)}, u32[]{:S(2)}, u32[]{:S(2)}) %all-to-all-start.1) | async-done | bytes 393248 | tf_op jit(solution)/shard_map/while/body/eval_jaxpr/all_to_all | solution.py:43
  1076.9 10.5 all-to-all-done
  1106.1 12.5 %all-to-all-done.1 = bf16[16,48,256]{2,1,0:T(8,128)(2,1)S(1)} async-done(((bf16[16,48,256]{2,1,0:T(8,128)(2,1)}), bf16[16,48,256]{2,1,0:T(8,128)(2,1)S(1)}, u32[]{:S(2)}, u32[]{:S(2)}) %all-to-all-start.1) | async-done | bytes 393248 | tf_op jit(solution)/shard_map/while/body/eval_jaxpr/all_to_all | solution.py:43
  1165.5 12.5 %all-to-all-done.1 = bf16[16,48,256]{2,1,0:T(8,128)(2,1)S(1)} async-done(((bf16[16,48,256]{2,1,0:T(8,128)(2,1)}), bf16[16,48,256]{2,1,0:T(8,128)(2,1)S(1)}, u32[]{:S(2)}, u32[]{:S(2)}) %all-to-all-start.1) | async-done | bytes 393248 | tf_op jit(solution)/shard_map/while/body/eval_jaxpr/all_to_all | solution.py:43
  (617 shorter events, 755.1 us)
Async XLA Ops:
  6.5 67.8 %all-gather.4.cloned.1.call-start = ((), (), s32[]{:S(2)}) async-start(), calls=%async_computation.3 | async-start | bytes 1253376 | tf_op jit(solution)/shard_map/all_gather | solution.py:114
  35.2 87.8 %all-gather.6.cloned.1.call-start = ((), (), s32[]{:S(2)}) async-start(), calls=%async_computation.4 | async-start | bytes 1253376 | tf_op jit(solution)/shard_map/all_gather | solution.py:22
  126.7 23.8 %all-to-all-start = ((bf16[16,48,256]{2,1,0:T(8,128)(2,1)}), bf16[16,48,256]{2,1,0:T(8,128)(2,1)S(1)}, u32[]{:S(2)}, u32[]{:S(2)}) async-start(bf16[16,48,256]{2,1,0:T(8,128)(2,1)} %broadcast_in_dim.123), calls=%async_computation | async-start | bytes 786432 | tf_op jit(solution)/shard_map/while/body/eval_jaxpr/all_to_all | solution.py:12
  164.3 17.4 %all-to-all-start.1 = ((bf16[16,48,256]{2,1,0:T(8,128)(2,1)}), bf16[16,48,256]{2,1,0:T(8,128)(2,1)S(1)}, u32[]{:S(2)}, u32[]{:S(2)}) async-start(bf16[16,48,256]{2,1,0:T(8,128)(2,1)} %bitcast.132), calls=%async_computation.1 | async-start | bytes 786432 | tf_op jit(solution)/shard_map/while/body/eval_jaxpr/all_to_all | solution.py:43
  188.4 18.3 %all-to-all-start = ((bf16[16,48,256]{2,1,0:T(8,128)(2,1)}), bf16[16,48,256]{2,1,0:T(8,128)(2,1)S(1)}, u32[]{:S(2)}, u32[]{:S(2)}) async-start(bf16[16,48,256]{2,1,0:T(8,128)(2,1)} %broadcast_in_dim.123), calls=%async_computation | async-start | bytes 786432 | tf_op jit(solution)/shard_map/while/body/eval_jaxpr/all_to_all | solution.py:12
  220.4 17.4 %all-to-all-start.1 = ((bf16[16,48,256]{2,1,0:T(8,128)(2,1)}), bf16[16,48,256]{2,1,0:T(8,128)(2,1)S(1)}, u32[]{:S(2)}, u32[]{:S(2)}) async-start(bf16[16,48,256]{2,1,0:T(8,128)(2,1)} %bitcast.132), calls=%async_computation.1 | async-start | bytes 786432 | tf_op jit(solution)/shard_map/while/body/eval_jaxpr/all_to_all | solution.py:43
  245.6 18.3 %all-to-all-start = ((bf16[16,48,256]{2,1,0:T(8,128)(2,1)}), bf16[16,48,256]{2,1,0:T(8,128)(2,1)S(1)}, u32[]{:S(2)}, u32[]{:S(2)}) async-start(bf16[16,48,256]{2,1,0:T(8,128)(2,1)} %broadcast_in_dim.123), calls=%async_computation | async-start | bytes 786432 | tf_op jit(solution)/shard_map/while/body/eval_jaxpr/all_to_all | solution.py:12
  302.8 18.3 %all-to-all-start = ((bf16[16,48,256]{2,1,0:T(8,128)(2,1)}), bf16[16,48,256]{2,1,0:T(8,128)(2,1)S(1)}, u32[]{:S(2)}, u32[]{:S(2)}) async-start(bf16[16,48,256]{2,1,0:T(8,128)(2,1)} %broadcast_in_dim.123), calls=%async_computation | async-start | bytes 786432 | tf_op jit(solution)/shard_map/while/body/eval_jaxpr/all_to_all | solution.py:12
  360.1 18.3 %all-to-all-start = ((bf16[16,48,256]{2,1,0:T(8,128)(2,1)}), bf16[16,48,256]{2,1,0:T(8,128)(2,1)S(1)}, u32[]{:S(2)}, u32[]{:S(2)}) async-start(bf16[16,48,256]{2,1,0:T(8,128)(2,1)} %broadcast_in_dim.123), calls=%async_computation | async-start | bytes 786432 | tf_op jit(solution)/shard_map/while/body/eval_jaxpr/all_to_all | solution.py:12
  392.1 17.4 %all-to-all-start.1 = ((bf16[16,48,256]{2,1,0:T(8,128)(2,1)}), bf16[16,48,256]{2,1,0:T(8,128)(2,1)S(1)}, u32[]{:S(2)}, u32[]{:S(2)}) async-start(bf16[16,48,256]{2,1,0:T(8,128)(2,1)} %bitcast.132), calls=%async_computation.1 | async-start | bytes 786432 | tf_op jit(solution)/shard_map/while/body/eval_jaxpr/all_to_all | solution.py:43
  417.3 18.3 %all-to-all-start = ((bf16[16,48,256]{2,1,0:T(8,128)(2,1)}), bf16[16,48,256]{2,1,0:T(8,128)(2,1)S(1)}, u32[]{:S(2)}, u32[]{:S(2)}) async-start(bf16[16,48,256]{2,1,0:T(8,128)(2,1)} %broadcast_in_dim.123), calls=%async_computation | async-start | bytes 786432 | tf_op jit(solution)/shard_map/while/body/eval_jaxpr/all_to_all | solution.py:12
  475.9 18.3 %all-to-all-start = ((bf16[16,48,256]{2,1,0:T(8,128)(2,1)}), bf16[16,48,256]{2,1,0:T(8,128)(2,1)S(1)}, u32[]{:S(2)}, u32[]{:S(2)}) async-start(bf16[16,48,256]{2,1,0:T(8,128)(2,1)} %broadcast_in_dim.123), calls=%async_computation | async-start | bytes 786432 | tf_op jit(solution)/shard_map/while/body/eval_jaxpr/all_to_all | solution.py:12
  508.0 17.4 %all-to-all-start.1 = ((bf16[16,48,256]{2,1,0:T(8,128)(2,1)}), bf16[16,48,256]{2,1,0:T(8,128)(2,1)S(1)}, u32[]{:S(2)}, u32[]{:S(2)}) async-start(bf16[16,48,256]{2,1,0:T(8,128)(2,1)} %bitcast.132), calls=%async_computation.1 | async-start | bytes 786432 | tf_op jit(solution)/shard_map/while/body/eval_jaxpr/all_to_all | solution.py:43
  535.2 18.3 %all-to-all-start = ((bf16[16,48,256]{2,1,0:T(8,128)(2,1)}), bf16[16,48,256]{2,1,0:T(8,128)(2,1)S(1)}, u32[]{:S(2)}, u32[]{:S(2)}) async-start(bf16[16,48,256]{2,1,0:T(8,128)(2,1)} %broadcast_in_dim.123), calls=%async_computation | async-start | bytes 786432 | tf_op jit(solution)/shard_map/while/body/eval_jaxpr/all_to_all | solution.py:12
  567.3 17.4 %all-to-all-start.1 = ((bf16[16,48,256]{2,1,0:T(8,128)(2,1)}), bf16[16,48,256]{2,1,0:T(8,128)(2,1)S(1)}, u32[]{:S(2)}, u32[]{:S(2)}) async-start(bf16[16,48,256]{2,1,0:T(8,128)(2,1)} %bitcast.132), calls=%async_computation.1 | async-start | bytes 786432 | tf_op jit(solution)/shard_map/while/body/eval_jaxpr/all_to_all | solution.py:43
  594.6 18.3 %all-to-all-start = ((bf16[16,48,256]{2,1,0:T(8,128)(2,1)}), bf16[16,48,256]{2,1,0:T(8,128)(2,1)S(1)}, u32[]{:S(2)}, u32[]{:S(2)}) async-start(bf16[16,48,256]{2,1,0:T(8,128)(2,1)} %broadcast_in_dim.123), calls=%async_computation | async-start | bytes 786432 | tf_op jit(solution)/shard_map/while/body/eval_jaxpr/all_to_all | solution.py:12
  626.6 17.4 %all-to-all-start.1 = ((bf16[16,48,256]{2,1,0:T(8,128)(2,1)}), bf16[16,48,256]{2,1,0:T(8,128)(2,1)S(1)}, u32[]{:S(2)}, u32[]{:S(2)}) async-start(bf16[16,48,256]{2,1,0:T(8,128)(2,1)} %bitcast.132), calls=%async_computation.1 | async-start | bytes 786432 | tf_op jit(solution)/shard_map/while/body/eval_jaxpr/all_to_all | solution.py:43
  653.9 18.3 %all-to-all-start = ((bf16[16,48,256]{2,1,0:T(8,128)(2,1)}), bf16[16,48,256]{2,1,0:T(8,128)(2,1)S(1)}, u32[]{:S(2)}, u32[]{:S(2)}) async-start(bf16[16,48,256]{2,1,0:T(8,128)(2,1)} %broadcast_in_dim.123), calls=%async_computation | async-start | bytes 786432 | tf_op jit(solution)/shard_map/while/body/eval_jaxpr/all_to_all | solution.py:12
  686.0 17.4 %all-to-all-start.1 = ((bf16[16,48,256]{2,1,0:T(8,128)(2,1)}), bf16[16,48,256]{2,1,0:T(8,128)(2,1)S(1)}, u32[]{:S(2)}, u32[]{:S(2)}) async-start(bf16[16,48,256]{2,1,0:T(8,128)(2,1)} %bitcast.132), calls=%async_computation.1 | async-start | bytes 786432 | tf_op jit(solution)/shard_map/while/body/eval_jaxpr/all_to_all | solution.py:43
  713.2 18.3 %all-to-all-start = ((bf16[16,48,256]{2,1,0:T(8,128)(2,1)}), bf16[16,48,256]{2,1,0:T(8,128)(2,1)S(1)}, u32[]{:S(2)}, u32[]{:S(2)}) async-start(bf16[16,48,256]{2,1,0:T(8,128)(2,1)} %broadcast_in_dim.123), calls=%async_computation | async-start | bytes 786432 | tf_op jit(solution)/shard_map/while/body/eval_jaxpr/all_to_all | solution.py:12
  745.3 17.4 %all-to-all-start.1 = ((bf16[16,48,256]{2,1,0:T(8,128)(2,1)}), bf16[16,48,256]{2,1,0:T(8,128)(2,1)S(1)}, u32[]{:S(2)}, u32[]{:S(2)}) async-start(bf16[16,48,256]{2,1,0:T(8,128)(2,1)} %bitcast.132), calls=%async_computation.1 | async-start | bytes 786432 | tf_op jit(solution)/shard_map/while/body/eval_jaxpr/all_to_all | solution.py:43
  772.6 18.3 %all-to-all-start = ((bf16[16,48,256]{2,1,0:T(8,128)(2,1)}), bf16[16,48,256]{2,1,0:T(8,128)(2,1)S(1)}, u32[]{:S(2)}, u32[]{:S(2)}) async-start(bf16[16,48,256]{2,1,0:T(8,128)(2,1)} %broadcast_in_dim.123), calls=%async_computation | async-start | bytes 786432 | tf_op jit(solution)/shard_map/while/body/eval_jaxpr/all_to_all | solution.py:12
  804.6 17.4 %all-to-all-start.1 = ((bf16[16,48,256]{2,1,0:T(8,128)(2,1)}), bf16[16,48,256]{2,1,0:T(8,128)(2,1)S(1)}, u32[]{:S(2)}, u32[]{:S(2)}) async-start(bf16[16,48,256]{2,1,0:T(8,128)(2,1)} %bitcast.132), calls=%async_computation.1 | async-start | bytes 786432 | tf_op jit(solution)/shard_map/while/body/eval_jaxpr/all_to_all | solution.py:43
  831.9 18.3 %all-to-all-start = ((bf16[16,48,256]{2,1,0:T(8,128)(2,1)}), bf16[16,48,256]{2,1,0:T(8,128)(2,1)S(1)}, u32[]{:S(2)}, u32[]{:S(2)}) async-start(bf16[16,48,256]{2,1,0:T(8,128)(2,1)} %broadcast_in_dim.123), calls=%async_computation | async-start | bytes 786432 | tf_op jit(solution)/shard_map/while/body/eval_jaxpr/all_to_all | solution.py:12
  891.2 18.3 %all-to-all-start = ((bf16[16,48,256]{2,1,0:T(8,128)(2,1)}), bf16[16,48,256]{2,1,0:T(8,128)(2,1)S(1)}, u32[]{:S(2)}, u32[]{:S(2)}) async-start(bf16[16,48,256]{2,1,0:T(8,128)(2,1)} %broadcast_in_dim.123), calls=%async_computation | async-start | bytes 786432 | tf_op jit(solution)/shard_map/while/body/eval_jaxpr/all_to_all | solution.py:12
  950.6 18.3 %all-to-all-start = ((bf16[16,48,256]{2,1,0:T(8,128)(2,1)}), bf16[16,48,256]{2,1,0:T(8,128)(2,1)S(1)}, u32[]{:S(2)}, u32[]{:S(2)}) async-start(bf16[16,48,256]{2,1,0:T(8,128)(2,1)} %broadcast_in_dim.123), calls=%async_computation | async-start | bytes 786432 | tf_op jit(solution)/shard_map/while/body/eval_jaxpr/all_to_all | solution.py:12
  982.6 17.4 %all-to-all-start.1 = ((bf16[16,48,256]{2,1,0:T(8,128)(2,1)}), bf16[16,48,256]{2,1,0:T(8,128)(2,1)S(1)}, u32[]{:S(2)}, u32[]{:S(2)}) async-start(bf16[16,48,256]{2,1,0:T(8,128)(2,1)} %bitcast.132), calls=%async_computation.1 | async-start | bytes 786432 | tf_op jit(solution)/shard_map/while/body/eval_jaxpr/all_to_all | solution.py:43
  1009.9 18.3 %all-to-all-start = ((bf16[16,48,256]{2,1,0:T(8,128)(2,1)}), bf16[16,48,256]{2,1,0:T(8,128)(2,1)S(1)}, u32[]{:S(2)}, u32[]{:S(2)}) async-start(bf16[16,48,256]{2,1,0:T(8,128)(2,1)} %broadcast_in_dim.123), calls=%async_computation | async-start | bytes 786432 | tf_op jit(solution)/shard_map/while/body/eval_jaxpr/all_to_all | solution.py:12
  1042.0 17.4 %all-to-all-start.1 = ((bf16[16,48,256]{2,1,0:T(8,128)(2,1)}), bf16[16,48,256]{2,1,0:T(8,128)(2,1)S(1)}, u32[]{:S(2)}, u32[]{:S(2)}) async-start(bf16[16,48,256]{2,1,0:T(8,128)(2,1)} %bitcast.132), calls=%async_computation.1 | async-start | bytes 786432 | tf_op jit(solution)/shard_map/while/body/eval_jaxpr/all_to_all | solution.py:43
  1069.2 18.3 %all-to-all-start = ((bf16[16,48,256]{2,1,0:T(8,128)(2,1)}), bf16[16,48,256]{2,1,0:T(8,128)(2,1)S(1)}, u32[]{:S(2)}, u32[]{:S(2)}) async-start(bf16[16,48,256]{2,1,0:T(8,128)(2,1)} %broadcast_in_dim.123), calls=%async_computation | async-start | bytes 786432 | tf_op jit(solution)/shard_map/while/body/eval_jaxpr/all_to_all | solution.py:12
  1101.3 17.4 %all-to-all-start.1 = ((bf16[16,48,256]{2,1,0:T(8,128)(2,1)}), bf16[16,48,256]{2,1,0:T(8,128)(2,1)S(1)}, u32[]{:S(2)}, u32[]{:S(2)}) async-start(bf16[16,48,256]{2,1,0:T(8,128)(2,1)} %bitcast.132), calls=%async_computation.1 | async-start | bytes 786432 | tf_op jit(solution)/shard_map/while/body/eval_jaxpr/all_to_all | solution.py:43
  1128.6 18.3 %all-to-all-start = ((bf16[16,48,256]{2,1,0:T(8,128)(2,1)}), bf16[16,48,256]{2,1,0:T(8,128)(2,1)S(1)}, u32[]{:S(2)}, u32[]{:S(2)}) async-start(bf16[16,48,256]{2,1,0:T(8,128)(2,1)} %broadcast_in_dim.123), calls=%async_computation | async-start | bytes 786432 | tf_op jit(solution)/shard_map/while/body/eval_jaxpr/all_to_all | solution.py:12
  (83 other events, 458.2 us)
Sparse Core Ops, SparseCore 0:
  35.4 38.9 all-gather.3
  81.3 41.6 all-gather.5
where the time goes:
time: 1220 us; the launch traced here: 1190 us
  waiting for transfers between devices  502 us (41%)
  starting transfers between devices  232 us (19%)
  matrix products  178 us (15%)
  local copies, waits for them, and re-layouts  128 us (10%)
  other arithmetic  113 us (9%)
  blocking collectives  24.9 us (2%)
  between operations  13.5 us (1%)
    all_to_all x18, waiting for transfers between devices, summed_on_arrival(): lax.all_to_all(pieces, axis, split_axis=0, concat_axis=0, tiled=True)  226 us
    all_to_all x18, waiting for transfers between devices, from_everyone(): lax.all_to_all(jnp.broadcast_to(array[None], (peers, *array.shape)), axis...  190 us
    ppermute x18, starting transfers between devices, shifted(): lax.ppermute(value, axis, [(source, source + steps) for source in range(f...  96.1 us
    all_to_all x18, starting transfers between devices, from_everyone(): lax.all_to_all(jnp.broadcast_to(array[None], (peers, *array.shape)), axis...  73.2 us
    all_to_all x18, starting transfers between devices, summed_on_arrival(): lax.all_to_all(pieces, axis, split_axis=0, concat_axis=0, tiled=True)  62.1 us
    dot_general x18, matrix products, attention_branch(): key_rows = jnp.dot(normed, w_key, preferred_element_type=jnp.float32)  44.8 us
    dot_general x18, matrix products, attend(): jnp.einsum('hqk,khd->qhd', attn_probs, mixed_values, preferred_element_ty...  41 us
    sub x18, matrix products, attend(): expo = jnp.exp(scores - row_top)  40 us
  transfers between devices with their start and end apart: 56, of which 56 were waited for; matrix products, arithmetic and copies ran while one was open for 9% of the time, Pallas kernels for 0%

commit v1 on v0

v1 whole, which is shorter than its diff:
```python
import functools

import jax
import jax.numpy as jnp
from jax import lax
from jax.experimental import pallas as pl
from jax.experimental.pallas import tpu as pltpu
from jax.sharding import PartitionSpec as P

EPSILON = 1e-05
ROTARY_BASE = 10000.0
HEAD_DIM = 128
VMEM = pltpu.VMEM
PIECES = 4


def rotary_tables(length):
    half_dim = HEAD_DIM // 2
    positions = jnp.arange(length, dtype=jnp.float32)
    frequency = ROTARY_BASE ** (-(jnp.arange(half_dim, dtype=jnp.float32) * 2.0) / HEAD_DIM)
    angles = positions[:, None] * frequency[None, :]
    cosine, sine = jnp.cos(angles), jnp.sin(angles)
    return (
        jnp.concatenate([cosine, cosine], axis=-1),
        jnp.concatenate([-sine, sine], axis=-1),
    )


def layer_kernel(
    flags, x_ref, gain_ref, source_ref, mix_ref, cos_ref, sin_ref, wq, wk, wv, wo,
    keep_ref, give_ref, carried_ref, normed, w_in, w_out, sem_in, sem_out,
):
    shards, length, width = x_ref.shape
    depth = shards * width
    rows = depth // PIECES
    core, is_first = flags[0], flags[1]

    def in_copy(piece, which):
        span = pl.ds(piece * rows, rows)
        source = (wq, wk, wv)[which]
        return pltpu.make_async_copy(
            source.at[span, :],
            w_in.at[span, pl.ds(which * width, width)],
            sem_in.at[piece, which],
        )

    out_copy = pltpu.make_async_copy(wo, w_out, sem_out)
    for piece in range(PIECES):
        for which in range(3):
            in_copy(piece, which).start()
    out_copy.start()

    square = jnp.zeros((length, width), jnp.float32)
    for j in range(shards):
        value = x_ref[j].astype(jnp.float32)
        square = square + value * value
    scale = lax.rsqrt(jnp.sum(square, axis=-1, keepdims=True) * (1.0 / depth) + EPSILON)
    for j in range(shards):
        value = x_ref[j].astype(jnp.float32) * scale * gain_ref[j][None, :]
        normed[:, j * width : (j + 1) * width] = value.astype(jnp.bfloat16)

    total = jnp.zeros((length, 3 * width), jnp.float32)
    for piece in range(PIECES):
        for which in range(3):
            in_copy(piece, which).wait()
        total = total + jnp.dot(
            normed[:, piece * rows : (piece + 1) * rows],
            w_in[piece * rows : (piece + 1) * rows, :],
            preferred_element_type=jnp.float32,
        )
    values = total[:, 2 * width :]
    source = jnp.where(is_first == 1, values.astype(jnp.bfloat16), source_ref[...])
    carried_ref[...] = source
    mix = mix_ref[...]
    mixed = (mix * values + (1.0 - mix) * source.astype(jnp.float32)).astype(jnp.bfloat16)
    cosine, sine = cos_ref[...], sin_ref[...]
    causal = lax.broadcasted_iota(jnp.int32, (length, length), 0) >= lax.broadcasted_iota(
        jnp.int32, (length, length), 1
    )

    def rotated(part):
        return (part * cosine + pltpu.roll(part, HEAD_DIM // 2, 1) * sine).astype(jnp.bfloat16)

    attended = []
    for head in range(width // HEAD_DIM):
        low = head * HEAD_DIM
        query = rotated(total[:, low : low + HEAD_DIM])
        key = rotated(total[:, width + low : width + low + HEAD_DIM])
        scores = lax.dot_general(
            query, key, (((1,), (1,)), ((), ())), preferred_element_type=jnp.float32
        ) * HEAD_DIM ** (-0.5)
        scores = jnp.where(causal, scores, -1e30)
        expo = jnp.exp(scores - jnp.max(scores, axis=-1, keepdims=True))
        probs = (expo / jnp.sum(expo, axis=-1, keepdims=True)).astype(jnp.bfloat16)
        attended.append(
            jnp.dot(
                probs, mixed[:, low : low + HEAD_DIM], preferred_element_type=jnp.float32
            ).astype(jnp.bfloat16)
        )
    attended = jnp.concatenate(attended, axis=-1)
    out_copy.wait()
    for chip in range(shards // 2):
        for target, side in ((give_ref, 1 - core), (keep_ref, core)):
            low = pl.multiple_of((2 * chip + side) * width, width)
            target[chip] = jnp.dot(
                attended, w_out[:, pl.ds(low, width)], preferred_element_type=jnp.float32
            ).astype(jnp.bfloat16)


def run_layer(flags, x, gain, source, mix, cosine, sine, wq, wk, wv, wo):
    shards, length, width = x.shape
    depth = shards * width
    full = pl.BlockSpec(memory_space=VMEM)
    anywhere = pl.BlockSpec(memory_space=pl.ANY)
    half = jax.ShapeDtypeStruct((shards // 2, length, width), jnp.bfloat16)
    return pl.pallas_call(
        layer_kernel,
        out_shape=(half, half, jax.ShapeDtypeStruct((length, width), jnp.bfloat16)),
        in_specs=[pl.BlockSpec(memory_space=pltpu.SMEM)] + [full] * 6 + [anywhere] * 4,
        out_specs=(full, full, full),
        scratch_shapes=[
            VMEM((length, depth), jnp.bfloat16),
            VMEM((depth, 3 * width), jnp.bfloat16),
            VMEM((width, depth), jnp.bfloat16),
            pltpu.SemaphoreType.DMA((PIECES, 3)),
            pltpu.SemaphoreType.DMA,
        ],
        compiler_params=pltpu.CompilerParams(vmem_limit_bytes=24 * 1024 * 1024),
        name="layer",
    )(flags, x, gain, source, mix, cosine, sine, wq, wk, wv, wo)


def close_kernel(flags, arrived_ref, rows_ref, first_ref, old_ref, send_ref, outputs_ref):
    is_last, following, micro, is_valid = flags[0], flags[1], flags[2], flags[3]
    summed = rows_ref[...].astype(jnp.float32)
    partial = arrived_ref[0].astype(jnp.float32)
    for j in range(1, arrived_ref.shape[0]):
        partial = partial + arrived_ref[j].astype(jnp.float32)
    fresh = (summed + partial).astype(jnp.bfloat16)
    send_ref[...] = jnp.where(is_last == 1, first_ref[following], fresh)
    for m in range(outputs_ref.shape[0]):
        outputs_ref[m] = jnp.where((micro == m) & (is_valid == 1), fresh, old_ref[m])


def close_layer(flags, arrived, rows, first, outputs):
    full = pl.BlockSpec(memory_space=VMEM)
    return pl.pallas_call(
        close_kernel,
        out_shape=(
            jax.ShapeDtypeStruct(rows.shape, jnp.bfloat16),
            jax.ShapeDtypeStruct(outputs.shape, jnp.bfloat16),
        ),
        in_specs=[pl.BlockSpec(memory_space=pltpu.SMEM)] + [full] * 4,
        out_specs=(full, full),
        compiler_params=pltpu.CompilerParams(vmem_limit_bytes=8 * 1024 * 1024),
        name="close",
    )(flags, arrived, rows, first, outputs)


def shards(
    token_ids, emb_table, attn_gain, query_weight, key_weight, value_weight, mix_weight, out_weight
):
    section_rank = lax.axis_index("section")
    section_count = lax.axis_size("section")
    tensor_rank = lax.axis_index("tensor")
    tensor_count = lax.axis_size("tensor")
    batches, length = token_ids.shape
    vocab_local, width = emb_table.shape
    chips = tensor_count // 2
    same_core = [[2 * chip + core for chip in range(chips)] for core in range(2)]
    gain = attn_gain[0].astype(jnp.float32).reshape(tensor_count, width)
    weights = (query_weight[0], key_weight[0], value_weight[0], out_weight[0])
    mix = jnp.repeat(mix_weight[0], HEAD_DIM)[None, :]
    cosine, sine = rotary_tables(length)
    is_first = (section_rank == 0).astype(jnp.int32)
    is_last = (section_rank == section_count - 1).astype(jnp.int32)
    layer_flags = jnp.stack([lax.rem(tensor_rank, 2), is_first]).astype(jnp.int32)

    flat_ids = token_ids.reshape(-1) - section_rank * vocab_local
    one_hot = (flat_ids[:, None] == jnp.arange(vocab_local, dtype=jnp.int32)[None, :]).astype(
        jnp.bfloat16
    )
    looked = jnp.dot(one_hot, emb_table, preferred_element_type=jnp.float32).astype(jnp.bfloat16)
    found = lax.all_to_all(
        jnp.broadcast_to(looked[None], (section_count, *looked.shape)), "section", 0, 0, tiled=True
    )
    first = found.astype(jnp.float32).sum(axis=0).astype(jnp.bfloat16)
    first = first.reshape(batches, length, width)
    ring = [(s, (s + 1) % section_count) for s in range(section_count)]
    partner = [(t, t ^ 1) for t in range(tensor_count)]

    def advance(step, state):
        rows, source, outputs = state
        position = step - section_rank
        is_valid = ((position >= 0) & (position < batches)).astype(jnp.int32)
        micro = jnp.clip(position, 0, batches - 1)
        following = jnp.minimum(step + 1, batches - 1)
        close_flags = jnp.stack([is_last, following, micro, is_valid]).astype(jnp.int32)
        full = lax.all_gather(rows, "tensor", axis=0, tiled=True)
        full = full.reshape(tensor_count, length, width)
        keep, give, carried = run_layer(
            layer_flags, full, gain, source, mix, cosine, sine, *weights
        )
        given = lax.ppermute(give, "tensor", partner)
        pair = (keep.astype(jnp.float32) + given.astype(jnp.float32)).astype(jnp.bfloat16)
        arrived = lax.all_to_all(pair, "tensor", 0, 0, axis_index_groups=same_core, tiled=True)
        send, outputs = close_layer(close_flags, arrived, rows, first, outputs)
        rows = lax.ppermute(send, "section", ring)
        source = lax.ppermute(carried, "section", ring)
        return rows, source, outputs

    source = jnp.zeros((length, width), jnp.bfloat16)
    outputs = jnp.zeros((batches, length, width), jnp.bfloat16)
    step_count = batches + section_count - 1
    _, _, outputs = lax.fori_loop(0, step_count, advance, (first[0], source, outputs))
    return outputs[None]


def solution(mesh):
    in_specs = (
        P(),
        P("section", "tensor"),
        P("section", None),
        P("section", None, "tensor"),
        P("section", None, "tensor"),
        P("section", None, "tensor"),
        P("section", "tensor"),
        P("section", "tensor", None),
    )
    out_specs = P("section", None, None, "tensor")
    return jax.shard_map(shards, mesh=mesh, in_specs=in_specs, out_specs=out_specs, check_vma=False)
```

time: 1220 us -> 872 us (0.71); the launches traced: 1190 us -> 868 us
  blocking collectives: 24.9 us -> 336 us
  waiting for transfers between devices: 502 us -> 303 us
  matrix products: 178 us -> 0.37 us
  starting transfers between devices: 232 us -> 75.5 us
  Pallas kernels: 0 us -> 114 us
  local copies, waits for them, and re-layouts: 128 us -> 20 us
  other arithmetic: 113 us -> 17.6 us
  between operations: 13.5 us -> 0.08 us
    all_gather x0 -> x18, blocking collectives: none -> 336 us  [advance(): full = lax.all_gather(rows, 'tensor', axis=0, tiled=True)]
    all_to_all x36 -> x19, waiting for transfers between devices: 416 us -> 172 us  [the longest x18 157 us: advance(): lax.all_to_all(pair, 'tensor', 0, 0, axis_index_groups=same_core, tiled=T...]
    dot_general x74 -> x1, matrix products: 138 us -> 0.37 us  [shards(): jnp.dot(one_hot, emb_table, preferred_element_type=jnp.float32)]
    pallas_call x0 -> x36, Pallas kernels: none -> 114 us  [the longest x18 92.4 us: run_layer(): pl.pallas_call(layer_kernel, out_shape=(half, half, jax.ShapeDtypeStruct(...]
    ppermute x18 -> x54, waiting for transfers between devices: 16.6 us -> 131 us  [the longest x18 108 us: advance(): rows = lax.ppermute(send, 'section', ring)]
    ppermute x18 -> x54, starting transfers between devices: 96.1 us -> 6.38 us  [the longest x18 4.45 us: advance(): given = lax.ppermute(give, 'tensor', partner)]
    all_gather x2 -> x0, waiting for transfers between devices: 69.6 us -> none  [the longest x1 36.1 us: shards(): first_full = lax.all_gather(first_shard, 'tensor', axis=1, tiled=True)]
    all_to_all x36 -> x19, starting transfers between devices: 135 us -> 69.1 us  [the longest x18 61.3 us: advance(): lax.all_to_all(pair, 'tensor', 0, 0, axis_index_groups=same_core, tiled=T...]
  transfers between devices with their start and end apart: 56 -> 73, of which waited for: 56 -> 55; matrix products, arithmetic and copies ran while one was open for 9% -> 2% of each run, Pallas kernels for 0% -> 3%
where the time goes in v1:
time: 872 us; the launch traced here: 868 us
  blocking collectives  336 us (39%)
  waiting for transfers between devices  303 us (35%)
  Pallas kernels  114 us (13%)
  starting transfers between devices  75.5 us (9%)
  local copies, waits for them, and re-layouts  20 us (2%)
  other arithmetic  17.6 us (2%)
    all_gather x18, blocking collectives, advance(): full = lax.all_gather(rows, 'tensor', axis=0, tiled=True)  336 us
    all_to_all x18, waiting for transfers between devices, advance(): lax.all_to_all(pair, 'tensor', 0, 0, axis_index_groups=same_core, tiled=T...  157 us
    ppermute x18, waiting for transfers between devices, advance(): rows = lax.ppermute(send, 'section', ring)  108 us
    pallas_call x18, Pallas kernels, run_layer(): pl.pallas_call(layer_kernel, out_shape=(half, half, jax.ShapeDtypeStruct(...  92.4 us
    all_to_all x18, starting transfers between devices, advance(): lax.all_to_all(pair, 'tensor', 0, 0, axis_index_groups=same_core, tiled=T...  61.3 us
    ppermute x18, waiting for transfers between devices, advance(): given = lax.ppermute(give, 'tensor', partner)  23.1 us
    pallas_call x18, Pallas kernels, close_layer(): pl.pallas_call(close_kernel, out_shape=(jax.ShapeDtypeStruct(rows.shape,...  21.8 us
  transfers between devices with their start and end apart: 73, of which 55 were waited for; matrix products, arithmetic and copies ran while one was open for 2% of the time, Pallas kernels for 3%

profile of v1, /device:TPU:1, one launch (start us, length us, event | category | flops | bytes accessed | tf_op | source)
XLA Modules:
  0.0 867.5 jit_solution(935274052024312719)
XLA Ops:
  12.1 15.5 %all-to-all-done.1 = bf16[16,144,256]{2,1,0:T(8,128)(2,1)} async-done(((bf16[16,144,256]{2,1,0:T(8,128)(2,1)}), bf16[16,144,256]{2,1,0:T(8,128)(2,1)}, u32[]{:S(2)}, u32[]{:S(2)}) %all-to-all-start.1) | async-done | bytes 1179680 | tf_op jit(solution)/shard_map/all_to_all | solution.py:184
  29.7 837.9 %while.18 = (s32[]{:T(128)}, bf16[48,256]{1,0:T(8,128)(2,1)S(1)}, bf16[48,256]{1,0:T(8,128)(2,1)S(1)}, bf16[3,48,256]{2,1,0:T(8,128)(2,1)}, s32[]{:T(128)}, /*in...) while((s32[]{:T(128)}, bf16[48,256]{1,0:T(8,128)(2,1)S(1)}, ...), condition=%wide.region_2.3_spmd.clone, body=%wide.region_1.2_spmd.clone.sunk | while | flops 393238 | bytes 2729407 | solution.py:215
  29.7 24.1 %all_gather.9 = bf16[768,256]{1,0:T(8,128)(2,1)S(1)} all-gather(bf16[48,256]{1,0:T(8,128)(2,1)S(1)} %get-tuple-element.448.rows_ref), channel_id=1, replica_groups=mesh['section'=16,'tensor'=16] {'tensor'}, dimensions={0}, use_global_device_ids=true | all-gather | bytes 417792 | tf_op jit(solution)/shard_map/while/body/eval_jaxpr/all_gather | solution.py:199
  81.6 18.4 %all_gather.9 = bf16[768,256]{1,0:T(8,128)(2,1)S(1)} all-gather(bf16[48,256]{1,0:T(8,128)(2,1)S(1)} %get-tuple-element.448.rows_ref), channel_id=1, replica_groups=mesh['section'=16,'tensor'=16] {'tensor'}, dimensions={0}, use_global_device_ids=true | all-gather | bytes 417792 | tf_op jit(solution)/shard_map/while/body/eval_jaxpr/all_gather | solution.py:199
  111.9 8.7 %all-to-all-done.arrived_ref = bf16[8,48,256]{2,1,0:T(8,128)(2,1)S(1)} async-done(((bf16[8,48,256]{2,1,0:T(8,128)(2,1)}), bf16[8,48,256]{2,1,0:T(8,128)(2,1)S(1)}, u32[]{:S(2)}, u32[]{:S(2)}) %all-to-all-start) | async-done | bytes 196640 | tf_op jit(solution)/shard_map/while/body/eval_jaxpr/all_to_all | solution.py:206
  127.8 18.4 %all_gather.9 = bf16[768,256]{1,0:T(8,128)(2,1)S(1)} all-gather(bf16[48,256]{1,0:T(8,128)(2,1)S(1)} %get-tuple-element.448.rows_ref), channel_id=1, replica_groups=mesh['section'=16,'tensor'=16] {'tensor'}, dimensions={0}, use_global_device_ids=true | all-gather | bytes 417792 | tf_op jit(solution)/shard_map/while/body/eval_jaxpr/all_gather | solution.py:199
  158.1 8.7 %all-to-all-done.arrived_ref = bf16[8,48,256]{2,1,0:T(8,128)(2,1)S(1)} async-done(((bf16[8,48,256]{2,1,0:T(8,128)(2,1)}), bf16[8,48,256]{2,1,0:T(8,128)(2,1)S(1)}, u32[]{:S(2)}, u32[]{:S(2)}) %all-to-all-start) | async-done | bytes 196640 | tf_op jit(solution)/shard_map/while/body/eval_jaxpr/all_to_all | solution.py:206
  174.1 18.4 %all_gather.9 = bf16[768,256]{1,0:T(8,128)(2,1)S(1)} all-gather(bf16[48,256]{1,0:T(8,128)(2,1)S(1)} %get-tuple-element.448.rows_ref), channel_id=1, replica_groups=mesh['section'=16,'tensor'=16] {'tensor'}, dimensions={0}, use_global_device_ids=true | all-gather | bytes 417792 | tf_op jit(solution)/shard_map/while/body/eval_jaxpr/all_gather | solution.py:199
  204.4 8.7 %all-to-all-done.arrived_ref = bf16[8,48,256]{2,1,0:T(8,128)(2,1)S(1)} async-done(((bf16[8,48,256]{2,1,0:T(8,128)(2,1)}), bf16[8,48,256]{2,1,0:T(8,128)(2,1)S(1)}, u32[]{:S(2)}, u32[]{:S(2)}) %all-to-all-start) | async-done | bytes 196640 | tf_op jit(solution)/shard_map/while/body/eval_jaxpr/all_to_all | solution.py:206
  220.3 18.4 %all_gather.9 = bf16[768,256]{1,0:T(8,128)(2,1)S(1)} all-gather(bf16[48,256]{1,0:T(8,128)(2,1)S(1)} %get-tuple-element.448.rows_ref), channel_id=1, replica_groups=mesh['section'=16,'tensor'=16] {'tensor'}, dimensions={0}, use_global_device_ids=true | all-gather | bytes 417792 | tf_op jit(solution)/shard_map/while/body/eval_jaxpr/all_gather | solution.py:199
  250.6 8.7 %all-to-all-done.arrived_ref = bf16[8,48,256]{2,1,0:T(8,128)(2,1)S(1)} async-done(((bf16[8,48,256]{2,1,0:T(8,128)(2,1)}), bf16[8,48,256]{2,1,0:T(8,128)(2,1)S(1)}, u32[]{:S(2)}, u32[]{:S(2)}) %all-to-all-start) | async-done | bytes 196640 | tf_op jit(solution)/shard_map/while/body/eval_jaxpr/all_to_all | solution.py:206
  266.5 18.4 %all_gather.9 = bf16[768,256]{1,0:T(8,128)(2,1)S(1)} all-gather(bf16[48,256]{1,0:T(8,128)(2,1)S(1)} %get-tuple-element.448.rows_ref), channel_id=1, replica_groups=mesh['section'=16,'tensor'=16] {'tensor'}, dimensions={0}, use_global_device_ids=true | all-gather | bytes 417792 | tf_op jit(solution)/shard_map/while/body/eval_jaxpr/all_gather | solution.py:199
  312.7 18.4 %all_gather.9 = bf16[768,256]{1,0:T(8,128)(2,1)S(1)} all-gather(bf16[48,256]{1,0:T(8,128)(2,1)S(1)} %get-tuple-element.448.rows_ref), channel_id=1, replica_groups=mesh['section'=16,'tensor'=16] {'tensor'}, dimensions={0}, use_global_device_ids=true | all-gather | bytes 417792 | tf_op jit(solution)/shard_map/while/body/eval_jaxpr/all_gather | solution.py:199
  359.0 18.4 %all_gather.9 = bf16[768,256]{1,0:T(8,128)(2,1)S(1)} all-gather(bf16[48,256]{1,0:T(8,128)(2,1)S(1)} %get-tuple-element.448.rows_ref), channel_id=1, replica_groups=mesh['section'=16,'tensor'=16] {'tensor'}, dimensions={0}, use_global_device_ids=true | all-gather | bytes 417792 | tf_op jit(solution)/shard_map/while/body/eval_jaxpr/all_gather | solution.py:199
  405.2 18.4 %all_gather.9 = bf16[768,256]{1,0:T(8,128)(2,1)S(1)} all-gather(bf16[48,256]{1,0:T(8,128)(2,1)S(1)} %get-tuple-element.448.rows_ref), channel_id=1, replica_groups=mesh['section'=16,'tensor'=16] {'tensor'}, dimensions={0}, use_global_device_ids=true | all-gather | bytes 417792 | tf_op jit(solution)/shard_map/while/body/eval_jaxpr/all_gather | solution.py:199
  451.4 18.4 %all_gather.9 = bf16[768,256]{1,0:T(8,128)(2,1)S(1)} all-gather(bf16[48,256]{1,0:T(8,128)(2,1)S(1)} %get-tuple-element.448.rows_ref), channel_id=1, replica_groups=mesh['section'=16,'tensor'=16] {'tensor'}, dimensions={0}, use_global_device_ids=true | all-gather | bytes 417792 | tf_op jit(solution)/shard_map/while/body/eval_jaxpr/all_gather | solution.py:199
  497.7 18.4 %all_gather.9 = bf16[768,256]{1,0:T(8,128)(2,1)S(1)} all-gather(bf16[48,256]{1,0:T(8,128)(2,1)S(1)} %get-tuple-element.448.rows_ref), channel_id=1, replica_groups=mesh['section'=16,'tensor'=16] {'tensor'}, dimensions={0}, use_global_device_ids=true | all-gather | bytes 417792 | tf_op jit(solution)/shard_map/while/body/eval_jaxpr/all_gather | solution.py:199
  528.0 8.7 %all-to-all-done.arrived_ref = bf16[8,48,256]{2,1,0:T(8,128)(2,1)S(1)} async-done(((bf16[8,48,256]{2,1,0:T(8,128)(2,1)}), bf16[8,48,256]{2,1,0:T(8,128)(2,1)S(1)}, u32[]{:S(2)}, u32[]{:S(2)}) %all-to-all-start) | async-done | bytes 196640 | tf_op jit(solution)/shard_map/while/body/eval_jaxpr/all_to_all | solution.py:206
  543.9 18.4 %all_gather.9 = bf16[768,256]{1,0:T(8,128)(2,1)S(1)} all-gather(bf16[48,256]{1,0:T(8,128)(2,1)S(1)} %get-tuple-element.448.rows_ref), channel_id=1, replica_groups=mesh['section'=16,'tensor'=16] {'tensor'}, dimensions={0}, use_global_device_ids=true | all-gather | bytes 417792 | tf_op jit(solution)/shard_map/while/body/eval_jaxpr/all_gather | solution.py:199
  574.2 8.7 %all-to-all-done.arrived_ref = bf16[8,48,256]{2,1,0:T(8,128)(2,1)S(1)} async-done(((bf16[8,48,256]{2,1,0:T(8,128)(2,1)}), bf16[8,48,256]{2,1,0:T(8,128)(2,1)S(1)}, u32[]{:S(2)}, u32[]{:S(2)}) %all-to-all-start) | async-done | bytes 196640 | tf_op jit(solution)/shard_map/while/body/eval_jaxpr/all_to_all | solution.py:206
  590.1 18.4 %all_gather.9 = bf16[768,256]{1,0:T(8,128)(2,1)S(1)} all-gather(bf16[48,256]{1,0:T(8,128)(2,1)S(1)} %get-tuple-element.448.rows_ref), channel_id=1, replica_groups=mesh['section'=16,'tensor'=16] {'tensor'}, dimensions={0}, use_global_device_ids=true | all-gather | bytes 417792 | tf_op jit(solution)/shard_map/while/body/eval_jaxpr/all_gather | solution.py:199
  620.4 8.7 %all-to-all-done.arrived_ref = bf16[8,48,256]{2,1,0:T(8,128)(2,1)S(1)} async-done(((bf16[8,48,256]{2,1,0:T(8,128)(2,1)}), bf16[8,48,256]{2,1,0:T(8,128)(2,1)S(1)}, u32[]{:S(2)}, u32[]{:S(2)}) %all-to-all-start) | async-done | bytes 196640 | tf_op jit(solution)/shard_map/while/body/eval_jaxpr/all_to_all | solution.py:206
  636.4 18.4 %all_gather.9 = bf16[768,256]{1,0:T(8,128)(2,1)S(1)} all-gather(bf16[48,256]{1,0:T(8,128)(2,1)S(1)} %get-tuple-element.448.rows_ref), channel_id=1, replica_groups=mesh['section'=16,'tensor'=16] {'tensor'}, dimensions={0}, use_global_device_ids=true | all-gather | bytes 417792 | tf_op jit(solution)/shard_map/while/body/eval_jaxpr/all_gather | solution.py:199
  666.7 8.7 %all-to-all-done.arrived_ref = bf16[8,48,256]{2,1,0:T(8,128)(2,1)S(1)} async-done(((bf16[8,48,256]{2,1,0:T(8,128)(2,1)}), bf16[8,48,256]{2,1,0:T(8,128)(2,1)S(1)}, u32[]{:S(2)}, u32[]{:S(2)}) %all-to-all-start) | async-done | bytes 196640 | tf_op jit(solution)/shard_map/while/body/eval_jaxpr/all_to_all | solution.py:206
  682.6 18.4 %all_gather.9 = bf16[768,256]{1,0:T(8,128)(2,1)S(1)} all-gather(bf16[48,256]{1,0:T(8,128)(2,1)S(1)} %get-tuple-element.448.rows_ref), channel_id=1, replica_groups=mesh['section'=16,'tensor'=16] {'tensor'}, dimensions={0}, use_global_device_ids=true | all-gather | bytes 417792 | tf_op jit(solution)/shard_map/while/body/eval_jaxpr/all_gather | solution.py:199
  712.9 8.7 %all-to-all-done.arrived_ref = bf16[8,48,256]{2,1,0:T(8,128)(2,1)S(1)} async-done(((bf16[8,48,256]{2,1,0:T(8,128)(2,1)}), bf16[8,48,256]{2,1,0:T(8,128)(2,1)S(1)}, u32[]{:S(2)}, u32[]{:S(2)}) %all-to-all-start) | async-done | bytes 196640 | tf_op jit(solution)/shard_map/while/body/eval_jaxpr/all_to_all | solution.py:206
  728.8 18.4 %all_gather.9 = bf16[768,256]{1,0:T(8,128)(2,1)S(1)} all-gather(bf16[48,256]{1,0:T(8,128)(2,1)S(1)} %get-tuple-element.448.rows_ref), channel_id=1, replica_groups=mesh['section'=16,'tensor'=16] {'tensor'}, dimensions={0}, use_global_device_ids=true | all-gather | bytes 417792 | tf_op jit(solution)/shard_map/while/body/eval_jaxpr/all_gather | solution.py:199
  759.1 8.7 %all-to-all-done.arrived_ref = bf16[8,48,256]{2,1,0:T(8,128)(2,1)S(1)} async-done(((bf16[8,48,256]{2,1,0:T(8,128)(2,1)}), bf16[8,48,256]{2,1,0:T(8,128)(2,1)S(1)}, u32[]{:S(2)}, u32[]{:S(2)}) %all-to-all-start) | async-done | bytes 196640 | tf_op jit(solution)/shard_map/while/body/eval_jaxpr/all_to_all | solution.py:206
  775.1 18.4 %all_gather.9 = bf16[768,256]{1,0:T(8,128)(2,1)S(1)} all-gather(bf16[48,256]{1,0:T(8,128)(2,1)S(1)} %get-tuple-element.448.rows_ref), channel_id=1, replica_groups=mesh['section'=16,'tensor'=16] {'tensor'}, dimensions={0}, use_global_device_ids=true | all-gather | bytes 417792 | tf_op jit(solution)/shard_map/while/body/eval_jaxpr/all_gather | solution.py:199
  805.4 8.7 %all-to-all-done.arrived_ref = bf16[8,48,256]{2,1,0:T(8,128)(2,1)S(1)} async-done(((bf16[8,48,256]{2,1,0:T(8,128)(2,1)}), bf16[8,48,256]{2,1,0:T(8,128)(2,1)S(1)}, u32[]{:S(2)}, u32[]{:S(2)}) %all-to-all-start) | async-done | bytes 196640 | tf_op jit(solution)/shard_map/while/body/eval_jaxpr/all_to_all | solution.py:206
  821.3 18.4 %all_gather.9 = bf16[768,256]{1,0:T(8,128)(2,1)S(1)} all-gather(bf16[48,256]{1,0:T(8,128)(2,1)S(1)} %get-tuple-element.448.rows_ref), channel_id=1, replica_groups=mesh['section'=16,'tensor'=16] {'tensor'}, dimensions={0}, use_global_device_ids=true | all-gather | bytes 417792 | tf_op jit(solution)/shard_map/while/body/eval_jaxpr/all_gather | solution.py:199
  851.6 8.7 %all-to-all-done.arrived_ref = bf16[8,48,256]{2,1,0:T(8,128)(2,1)S(1)} async-done(((bf16[8,48,256]{2,1,0:T(8,128)(2,1)}), bf16[8,48,256]{2,1,0:T(8,128)(2,1)S(1)}, u32[]{:S(2)}, u32[]{:S(2)}) %all-to-all-start) | async-done | bytes 196640 | tf_op jit(solution)/shard_map/while/body/eval_jaxpr/all_to_all | solution.py:206
  (263 shorter events, 410.3 us)
Async XLA Ops:
  2.7 24.8 %all-to-all-start.1 = ((bf16[16,144,256]{2,1,0:T(8,128)(2,1)}), bf16[16,144,256]{2,1,0:T(8,128)(2,1)}, u32[]{:S(2)}, u32[]{:S(2)}) async-start(bf16[16,144,256]{2,1,0:T(8,128)(2,1)} %broadcast_in_dim.10), calls=%async_computation.1 | async-start | bytes 2359296 | tf_op jit(solution)/shard_map/all_to_all | solution.py:184
  61.2 13.1 %all-to-all-start = ((bf16[8,48,256]{2,1,0:T(8,128)(2,1)}), bf16[8,48,256]{2,1,0:T(8,128)(2,1)S(1)}, u32[]{:S(2)}, u32[]{:S(2)}) async-start(bf16[8,48,256]{2,1,0:T(8,128)(2,1)} %add_convert_fusion.2), calls=%async_computation | async-start | bytes 393216 | tf_op jit(solution)/shard_map/while/body/eval_jaxpr/all_to_all | solution.py:206
  64.6 11.2 %collective-permute-start.2 = (bf16[48,256]{1,0:T(8,128)(2,1)S(1)}, bf16[48,256]{1,0:T(8,128)(2,1)S(1)}, u32[]{:S(2)}, u32[]{:S(2)}) collective-permute-start(bf16[48,256]{1,0:T(8,128)(2,1)S(1)} %get-tuple-element.425), channel_id=1, source_target_pairs={{0,16},{16,32},{32,48},{48,64},{64,80},{80,96},{96,112},{112,128},... | collective-permute-start | bytes 73736 | tf_op jit(solution)/shard_map/while/body/eval_jaxpr/ppermute | solution.py:209
  107.4 13.2 %all-to-all-start = ((bf16[8,48,256]{2,1,0:T(8,128)(2,1)}), bf16[8,48,256]{2,1,0:T(8,128)(2,1)S(1)}, u32[]{:S(2)}, u32[]{:S(2)}) async-start(bf16[8,48,256]{2,1,0:T(8,128)(2,1)} %add_convert_fusion.2), calls=%async_computation | async-start | bytes 393216 | tf_op jit(solution)/shard_map/while/body/eval_jaxpr/all_to_all | solution.py:206
  110.8 11.0 %collective-permute-start.2 = (bf16[48,256]{1,0:T(8,128)(2,1)S(1)}, bf16[48,256]{1,0:T(8,128)(2,1)S(1)}, u32[]{:S(2)}, u32[]{:S(2)}) collective-permute-start(bf16[48,256]{1,0:T(8,128)(2,1)S(1)} %get-tuple-element.425), channel_id=1, source_target_pairs={{0,16},{16,32},{32,48},{48,64},{64,80},{80,96},{96,112},{112,128},... | collective-permute-start | bytes 73736 | tf_op jit(solution)/shard_map/while/body/eval_jaxpr/ppermute | solution.py:209
  153.6 13.2 %all-to-all-start = ((bf16[8,48,256]{2,1,0:T(8,128)(2,1)}), bf16[8,48,256]{2,1,0:T(8,128)(2,1)S(1)}, u32[]{:S(2)}, u32[]{:S(2)}) async-start(bf16[8,48,256]{2,1,0:T(8,128)(2,1)} %add_convert_fusion.2), calls=%async_computation | async-start | bytes 393216 | tf_op jit(solution)/shard_map/while/body/eval_jaxpr/all_to_all | solution.py:206
  157.1 11.0 %collective-permute-start.2 = (bf16[48,256]{1,0:T(8,128)(2,1)S(1)}, bf16[48,256]{1,0:T(8,128)(2,1)S(1)}, u32[]{:S(2)}, u32[]{:S(2)}) collective-permute-start(bf16[48,256]{1,0:T(8,128)(2,1)S(1)} %get-tuple-element.425), channel_id=1, source_target_pairs={{0,16},{16,32},{32,48},{48,64},{64,80},{80,96},{96,112},{112,128},... | collective-permute-start | bytes 73736 | tf_op jit(solution)/shard_map/while/body/eval_jaxpr/ppermute | solution.py:209
  199.9 13.2 %all-to-all-start = ((bf16[8,48,256]{2,1,0:T(8,128)(2,1)}), bf16[8,48,256]{2,1,0:T(8,128)(2,1)S(1)}, u32[]{:S(2)}, u32[]{:S(2)}) async-start(bf16[8,48,256]{2,1,0:T(8,128)(2,1)} %add_convert_fusion.2), calls=%async_computation | async-start | bytes 393216 | tf_op jit(solution)/shard_map/while/body/eval_jaxpr/all_to_all | solution.py:206
  203.3 11.0 %collective-permute-start.2 = (bf16[48,256]{1,0:T(8,128)(2,1)S(1)}, bf16[48,256]{1,0:T(8,128)(2,1)S(1)}, u32[]{:S(2)}, u32[]{:S(2)}) collective-permute-start(bf16[48,256]{1,0:T(8,128)(2,1)S(1)} %get-tuple-element.425), channel_id=1, source_target_pairs={{0,16},{16,32},{32,48},{48,64},{64,80},{80,96},{96,112},{112,128},... | collective-permute-start | bytes 73736 | tf_op jit(solution)/shard_map/while/body/eval_jaxpr/ppermute | solution.py:209
  246.1 13.2 %all-to-all-start = ((bf16[8,48,256]{2,1,0:T(8,128)(2,1)}), bf16[8,48,256]{2,1,0:T(8,128)(2,1)S(1)}, u32[]{:S(2)}, u32[]{:S(2)}) async-start(bf16[8,48,256]{2,1,0:T(8,128)(2,1)} %add_convert_fusion.2), calls=%async_computation | async-start | bytes 393216 | tf_op jit(solution)/shard_map/while/body/eval_jaxpr/all_to_all | solution.py:206
  249.5 11.0 %collective-permute-start.2 = (bf16[48,256]{1,0:T(8,128)(2,1)S(1)}, bf16[48,256]{1,0:T(8,128)(2,1)S(1)}, u32[]{:S(2)}, u32[]{:S(2)}) collective-permute-start(bf16[48,256]{1,0:T(8,128)(2,1)S(1)} %get-tuple-element.425), channel_id=1, source_target_pairs={{0,16},{16,32},{32,48},{48,64},{64,80},{80,96},{96,112},{112,128},... | collective-permute-start | bytes 73736 | tf_op jit(solution)/shard_map/while/body/eval_jaxpr/ppermute | solution.py:209
  292.3 13.2 %all-to-all-start = ((bf16[8,48,256]{2,1,0:T(8,128)(2,1)}), bf16[8,48,256]{2,1,0:T(8,128)(2,1)S(1)}, u32[]{:S(2)}, u32[]{:S(2)}) async-start(bf16[8,48,256]{2,1,0:T(8,128)(2,1)} %add_convert_fusion.2), calls=%async_computation | async-start | bytes 393216 | tf_op jit(solution)/shard_map/while/body/eval_jaxpr/all_to_all | solution.py:206
  295.8 11.0 %collective-permute-start.2 = (bf16[48,256]{1,0:T(8,128)(2,1)S(1)}, bf16[48,256]{1,0:T(8,128)(2,1)S(1)}, u32[]{:S(2)}, u32[]{:S(2)}) collective-permute-start(bf16[48,256]{1,0:T(8,128)(2,1)S(1)} %get-tuple-element.425), channel_id=1, source_target_pairs={{0,16},{16,32},{32,48},{48,64},{64,80},{80,96},{96,112},{112,128},... | collective-permute-start | bytes 73736 | tf_op jit(solution)/shard_map/while/body/eval_jaxpr/ppermute | solution.py:209
  338.6 13.2 %all-to-all-start = ((bf16[8,48,256]{2,1,0:T(8,128)(2,1)}), bf16[8,48,256]{2,1,0:T(8,128)(2,1)S(1)}, u32[]{:S(2)}, u32[]{:S(2)}) async-start(bf16[8,48,256]{2,1,0:T(8,128)(2,1)} %add_convert_fusion.2), calls=%async_computation | async-start | bytes 393216 | tf_op jit(solution)/shard_map/while/body/eval_jaxpr/all_to_all | solution.py:206
  342.0 11.0 %collective-permute-start.2 = (bf16[48,256]{1,0:T(8,128)(2,1)S(1)}, bf16[48,256]{1,0:T(8,128)(2,1)S(1)}, u32[]{:S(2)}, u32[]{:S(2)}) collective-permute-start(bf16[48,256]{1,0:T(8,128)(2,1)S(1)} %get-tuple-element.425), channel_id=1, source_target_pairs={{0,16},{16,32},{32,48},{48,64},{64,80},{80,96},{96,112},{112,128},... | collective-permute-start | bytes 73736 | tf_op jit(solution)/shard_map/while/body/eval_jaxpr/ppermute | solution.py:209
  384.8 13.2 %all-to-all-start = ((bf16[8,48,256]{2,1,0:T(8,128)(2,1)}), bf16[8,48,256]{2,1,0:T(8,128)(2,1)S(1)}, u32[]{:S(2)}, u32[]{:S(2)}) async-start(bf16[8,48,256]{2,1,0:T(8,128)(2,1)} %add_convert_fusion.2), calls=%async_computation | async-start | bytes 393216 | tf_op jit(solution)/shard_map/while/body/eval_jaxpr/all_to_all | solution.py:206
  388.2 11.0 %collective-permute-start.2 = (bf16[48,256]{1,0:T(8,128)(2,1)S(1)}, bf16[48,256]{1,0:T(8,128)(2,1)S(1)}, u32[]{:S(2)}, u32[]{:S(2)}) collective-permute-start(bf16[48,256]{1,0:T(8,128)(2,1)S(1)} %get-tuple-element.425), channel_id=1, source_target_pairs={{0,16},{16,32},{32,48},{48,64},{64,80},{80,96},{96,112},{112,128},... | collective-permute-start | bytes 73736 | tf_op jit(solution)/shard_map/while/body/eval_jaxpr/ppermute | solution.py:209
  431.0 13.2 %all-to-all-start = ((bf16[8,48,256]{2,1,0:T(8,128)(2,1)}), bf16[8,48,256]{2,1,0:T(8,128)(2,1)S(1)}, u32[]{:S(2)}, u32[]{:S(2)}) async-start(bf16[8,48,256]{2,1,0:T(8,128)(2,1)} %add_convert_fusion.2), calls=%async_computation | async-start | bytes 393216 | tf_op jit(solution)/shard_map/while/body/eval_jaxpr/all_to_all | solution.py:206
  434.4 11.0 %collective-permute-start.2 = (bf16[48,256]{1,0:T(8,128)(2,1)S(1)}, bf16[48,256]{1,0:T(8,128)(2,1)S(1)}, u32[]{:S(2)}, u32[]{:S(2)}) collective-permute-start(bf16[48,256]{1,0:T(8,128)(2,1)S(1)} %get-tuple-element.425), channel_id=1, source_target_pairs={{0,16},{16,32},{32,48},{48,64},{64,80},{80,96},{96,112},{112,128},... | collective-permute-start | bytes 73736 | tf_op jit(solution)/shard_map/while/body/eval_jaxpr/ppermute | solution.py:209
  477.3 13.2 %all-to-all-start = ((bf16[8,48,256]{2,1,0:T(8,128)(2,1)}), bf16[8,48,256]{2,1,0:T(8,128)(2,1)S(1)}, u32[]{:S(2)}, u32[]{:S(2)}) async-start(bf16[8,48,256]{2,1,0:T(8,128)(2,1)} %add_convert_fusion.2), calls=%async_computation | async-start | bytes 393216 | tf_op jit(solution)/shard_map/while/body/eval_jaxpr/all_to_all | solution.py:206
  480.7 11.0 %collective-permute-start.2 = (bf16[48,256]{1,0:T(8,128)(2,1)S(1)}, bf16[48,256]{1,0:T(8,128)(2,1)S(1)}, u32[]{:S(2)}, u32[]{:S(2)}) collective-permute-start(bf16[48,256]{1,0:T(8,128)(2,1)S(1)} %get-tuple-element.425), channel_id=1, source_target_pairs={{0,16},{16,32},{32,48},{48,64},{64,80},{80,96},{96,112},{112,128},... | collective-permute-start | bytes 73736 | tf_op jit(solution)/shard_map/while/body/eval_jaxpr/ppermute | solution.py:209
  523.5 13.2 %all-to-all-start = ((bf16[8,48,256]{2,1,0:T(8,128)(2,1)}), bf16[8,48,256]{2,1,0:T(8,128)(2,1)S(1)}, u32[]{:S(2)}, u32[]{:S(2)}) async-start(bf16[8,48,256]{2,1,0:T(8,128)(2,1)} %add_convert_fusion.2), calls=%async_computation | async-start | bytes 393216 | tf_op jit(solution)/shard_map/while/body/eval_jaxpr/all_to_all | solution.py:206
  526.9 11.0 %collective-permute-start.2 = (bf16[48,256]{1,0:T(8,128)(2,1)S(1)}, bf16[48,256]{1,0:T(8,128)(2,1)S(1)}, u32[]{:S(2)}, u32[]{:S(2)}) collective-permute-start(bf16[48,256]{1,0:T(8,128)(2,1)S(1)} %get-tuple-element.425), channel_id=1, source_target_pairs={{0,16},{16,32},{32,48},{48,64},{64,80},{80,96},{96,112},{112,128},... | collective-permute-start | bytes 73736 | tf_op jit(solution)/shard_map/while/body/eval_jaxpr/ppermute | solution.py:209
  569.7 13.2 %all-to-all-start = ((bf16[8,48,256]{2,1,0:T(8,128)(2,1)}), bf16[8,48,256]{2,1,0:T(8,128)(2,1)S(1)}, u32[]{:S(2)}, u32[]{:S(2)}) async-start(bf16[8,48,256]{2,1,0:T(8,128)(2,1)} %add_convert_fusion.2), calls=%async_computation | async-start | bytes 393216 | tf_op jit(solution)/shard_map/while/body/eval_jaxpr/all_to_all | solution.py:206
  573.1 11.0 %collective-permute-start.2 = (bf16[48,256]{1,0:T(8,128)(2,1)S(1)}, bf16[48,256]{1,0:T(8,128)(2,1)S(1)}, u32[]{:S(2)}, u32[]{:S(2)}) collective-permute-start(bf16[48,256]{1,0:T(8,128)(2,1)S(1)} %get-tuple-element.425), channel_id=1, source_target_pairs={{0,16},{16,32},{32,48},{48,64},{64,80},{80,96},{96,112},{112,128},... | collective-permute-start | bytes 73736 | tf_op jit(solution)/shard_map/while/body/eval_jaxpr/ppermute | solution.py:209
  616.0 13.2 %all-to-all-start = ((bf16[8,48,256]{2,1,0:T(8,128)(2,1)}), bf16[8,48,256]{2,1,0:T(8,128)(2,1)S(1)}, u32[]{:S(2)}, u32[]{:S(2)}) async-start(bf16[8,48,256]{2,1,0:T(8,128)(2,1)} %add_convert_fusion.2), calls=%async_computation | async-start | bytes 393216 | tf_op jit(solution)/shard_map/while/body/eval_jaxpr/all_to_all | solution.py:206
  619.4 11.0 %collective-permute-start.2 = (bf16[48,256]{1,0:T(8,128)(2,1)S(1)}, bf16[48,256]{1,0:T(8,128)(2,1)S(1)}, u32[]{:S(2)}, u32[]{:S(2)}) collective-permute-start(bf16[48,256]{1,0:T(8,128)(2,1)S(1)} %get-tuple-element.425), channel_id=1, source_target_pairs={{0,16},{16,32},{32,48},{48,64},{64,80},{80,96},{96,112},{112,128},... | collective-permute-start | bytes 73736 | tf_op jit(solution)/shard_map/while/body/eval_jaxpr/ppermute | solution.py:209
  662.2 13.2 %all-to-all-start = ((bf16[8,48,256]{2,1,0:T(8,128)(2,1)}), bf16[8,48,256]{2,1,0:T(8,128)(2,1)S(1)}, u32[]{:S(2)}, u32[]{:S(2)}) async-start(bf16[8,48,256]{2,1,0:T(8,128)(2,1)} %add_convert_fusion.2), calls=%async_computation | async-start | bytes 393216 | tf_op jit(solution)/shard_map/while/body/eval_jaxpr/all_to_all | solution.py:206
  708.4 13.2 %all-to-all-start = ((bf16[8,48,256]{2,1,0:T(8,128)(2,1)}), bf16[8,48,256]{2,1,0:T(8,128)(2,1)S(1)}, u32[]{:S(2)}, u32[]{:S(2)}) async-start(bf16[8,48,256]{2,1,0:T(8,128)(2,1)} %add_convert_fusion.2), calls=%async_computation | async-start | bytes 393216 | tf_op jit(solution)/shard_map/while/body/eval_jaxpr/all_to_all | solution.py:206
  754.7 13.2 %all-to-all-start = ((bf16[8,48,256]{2,1,0:T(8,128)(2,1)}), bf16[8,48,256]{2,1,0:T(8,128)(2,1)S(1)}, u32[]{:S(2)}, u32[]{:S(2)}) async-start(bf16[8,48,256]{2,1,0:T(8,128)(2,1)} %add_convert_fusion.2), calls=%async_computation | async-start | bytes 393216 | tf_op jit(solution)/shard_map/while/body/eval_jaxpr/all_to_all | solution.py:206
  800.9 13.2 %all-to-all-start = ((bf16[8,48,256]{2,1,0:T(8,128)(2,1)}), bf16[8,48,256]{2,1,0:T(8,128)(2,1)S(1)}, u32[]{:S(2)}, u32[]{:S(2)}) async-start(bf16[8,48,256]{2,1,0:T(8,128)(2,1)} %add_convert_fusion.2), calls=%async_computation | async-start | bytes 393216 | tf_op jit(solution)/shard_map/while/body/eval_jaxpr/all_to_all | solution.py:206
  847.1 13.2 %all-to-all-start = ((bf16[8,48,256]{2,1,0:T(8,128)(2,1)}), bf16[8,48,256]{2,1,0:T(8,128)(2,1)S(1)}, u32[]{:S(2)}, u32[]{:S(2)}) async-start(bf16[8,48,256]{2,1,0:T(8,128)(2,1)} %add_convert_fusion.2), calls=%async_computation | async-start | bytes 393216 | tf_op jit(solution)/shard_map/while/body/eval_jaxpr/all_to_all | solution.py:206
  (45 other events, 254.5 us)
